TPU v7x, 256 devices: a whole 4x4x8 slice. The times are simulated.
256 devices in a mesh: aa: 8 (over y, core), ba: 4 (over x), col: 8 (over z).
Axes of the slice: x: 4, y: 4, z: 8, core: 2. Of those that a mesh axis runs over, the one named last changes fastest.
Arguments:
- hidden: bfloat16 [8, 4, 32, 8192], P('aa', 'ba', None, 'col'), may hold values from -36 to 60, as said below
- unembed: bfloat16 [8192, 152064], P(None, ('aa', 'ba', 'col')), may hold values from -1 to 5, as said below
- targets: int32 [8, 4, 32], replicated, may hold values from 0 to 152063
- lengths: int32 [8, 4], replicated, may hold values from 1 to 32
Outputs:
- scores: float32 [8, 4], P('aa', 'ba')
Inputs may be any that keep to these rules, and one draw needn't show every extreme that they name: real-valued hidden states. `unembed`: real-valued unembedding entries.
All inputs are finite; a program needn't handle non-finite values.
Results may differ from a plain program's by a relative error of at most 0.0003.
Values may be sent and summed in bfloat16 or wider, within the bound.
A program may use at most 128 MiB of HBM per device.

v0:
```python
import jax
import jax.numpy as jnp
from jax import lax
from jax.sharding import Mesh
from jax.sharding import PartitionSpec as P

AA = ("aa_0", "aa_1")
AA_BA_COL = ("aa_0", "aa_1", "ba", "col")
AA_BA = ("aa_0", "aa_1", "ba")


def in_order(parts, dim):
    parts = jnp.moveaxis(parts, 0, dim)
    dims = parts.shape
    return parts.reshape(*dims[:dim], dims[dim] * dims[dim + 1], *dims[dim + 2 :])


def copy_for_each(x, axis):
    copies = jnp.broadcast_to(x, (lax.axis_size(axis), *x.shape))
    return lax.all_to_all(copies, axis, split_axis=0, concat_axis=0, tiled=True)


def gather_directly(x, axis, dim):
    return in_order(copy_for_each(x, axis), dim)


def gathered_once(x, axis):
    leaves = jax.tree.leaves(x)
    turns = sorted(range(len(leaves)), key=lambda k: -leaves[k].size)
    width = (1, *leaves[turns[0]].shape)[-1]
    lines = [
        jnp.pad(leaves[k].reshape(-1), (0, -leaves[k].size % width)).reshape(-1, width)
        for k in turns
    ]
    both, at, found = (lax.all_gather(jnp.concatenate(lines), axis), 0, {})
    for k, line in zip(turns, lines):
        slab = both[:, at : at + len(line)].reshape(len(both), -1)
        found[k] = slab[:, : leaves[k].size].reshape(-1, *leaves[k].shape)
        at += len(line)
    numbers = iter(range(len(leaves)))
    return jax.tree.map(lambda _: found[next(numbers)], x)


def merged_by_axis(x, axes, combine):
    for axis in axes:
        pieces = gathered_once(x, axis)
        x = jax.tree.map(lambda part: part[0], pieces)
        for k in range(1, lax.axis_size(axis)):
            x = combine(x, jax.tree.map(lambda part: part[k], pieces))
    return x


def combine_stats(earlier, later):
    top_one, total_one, picked_one = earlier
    top_two, total_two, picked_two = later
    joined = jnp.maximum(top_one, top_two)
    total = total_one * jnp.exp(top_one - joined) + total_two * jnp.exp(top_two - joined)
    return (joined, total, picked_one + picked_two)


def body(hidden, unembed, targets, lengths):
    groups = lax.axis_size(AA)
    members = lax.axis_size("ba")
    per_group, choices_dev, seq_len, width_part = hidden.shape
    block_rows = per_group * choices_dev * seq_len
    own_rows = hidden.reshape(block_rows, width_part)
    vocab_part = unembed.shape[1]
    device_index = lax.axis_index(AA_BA_COL)
    offset = device_index * vocab_part
    full_rows = gather_directly(own_rows, "col", 1)
    logits = jnp.dot(
        lax.all_gather(full_rows, AA_BA, axis=0, tiled=True),
        unembed,
        preferred_element_type=jnp.float32,
    )
    ordered = targets.reshape(groups, per_group, members, seq_len).transpose(0, 2, 1, 3).reshape(-1)
    local_ids = ordered - offset
    columns = jnp.arange(vocab_part, dtype=jnp.int32)
    picked_part = jnp.sum(jnp.where(local_ids[:, None] == columns[None, :], logits, 0.0), axis=1)
    group_index = lax.axis_index(AA)
    member_index = lax.axis_index("ba")
    own_len = lax.dynamic_slice(lengths, (group_index * per_group, member_index), (per_group, 1))
    positions = jnp.arange(seq_len, dtype=jnp.int32)
    local_top = jnp.max(logits, axis=1)
    relative = jnp.sum(jnp.exp(logits - local_top[:, None]), axis=1)
    top, total, picked = merged_by_axis(
        (local_top, relative, picked_part), AA_BA_COL, combine_stats
    )
    first = (group_index * members + member_index) * block_rows
    mine = lax.dynamic_slice_in_dim(picked - top - jnp.log(total), first, block_rows).reshape(
        per_group, seq_len
    )
    valid = positions[None, :] < own_len
    summed = jnp.sum(jnp.where(valid, mine, 0.0), axis=1)
    return (summed / own_len[:, 0].astype(jnp.float32))[:, None]


def solution(mesh):
    split = Mesh(
        mesh.devices.reshape(4, 2, mesh.shape["ba"], mesh.shape["col"]),
        ("aa_0", "aa_1", "ba", "col"),
    )
    in_specs = (P(AA, "ba", None, "col"), P(None, AA_BA_COL), P(), P())
    out_specs = P(AA, "ba")
    return jax.shard_map(body, mesh=split, in_specs=in_specs, out_specs=out_specs, check_vma=False)
```

profile of v0, /device:TPU:2, one launch (start us, length us, event | category | flops | bytes accessed | tf_op | source)
XLA Modules:
  0.0 185.8 jit_solution(12175652836842939492)
XLA Ops:
  6.5 0.0 copy-start
  6.5 0.0 all-gather.10.cloned.1.call-start
  6.5 0.9 broadcast_in_dim.18
  7.4 25.8 %all_to_all.5 = bf16[8,32,1024]{2,1,0:T(8,128)(2,1)S(1)} all-to-all(bf16[8,32,1024]{2,1,0:T(8,128)(2,1)S(1)} %broadcast_in_dim.18), channel_id=1, replica_groups=mesh['aa_0'=4,'aa_1'=2,'ba'=4,'col'=8] {'col'}, dimensions={0} | all-to-all | bytes 1048576 | tf_op jit(solution)/shard_map/all_to_all | solution.py:20
  33.2 0.8 copy.6
  34.0 0.0 all-gather.10.cloned.1.call-update
  34.1 0.0 copy-done
  34.1 0.1 sub.213
  34.2 1.3 dynamic_slice.6
  36.1 72.0 %all-gather.10.cloned.1.call-done = bf16[1024,8192]{1,0:T(8,128)(2,1)} async-done(((bf16[32,8192]{1,0:T(8,128)(2,1)}), bf16[1024,8192]{1,0:T(8,128)(2,1)}) %all-gather.10.cloned.1.call-update) | async-done | bytes 16777232 | tf_op jit(solution)/shard_map/all_gather | solution.py:72
  108.1 15.5 %fusion.49 = (f32[1024]{0:T(1024)S(1)}, f32[1024,594]{0,1:T(8,128)S(1)}) fusion(bf16[1024,8192]{1,0:T(8,128)(2,1)} %all-gather.10.cloned.1.call-done, bf16[8192,594]{0,1:T(8,128)(2,1)} %param.5), kind=kOutput, calls=%fused_computation.97 | convolution fusion | flops 9966273536 | bytes 28946432 | tf_op jit(solution)/shard_map/dot_general | solution.py:71
  123.6 0.7 exponential_reduce_fusion
  124.3 11.9 %all-gather.4 = f32[4,3,1024]{2,1,0:T(4,128)S(1)} all-gather(f32[1,3,1024]{2,1,0:T(4,128)S(1)} %maximum_bitcast_fusion), channel_id=2, replica_groups=mesh['aa_0'=4,'aa_1'=2,'ba'=4,'col'=8] {'aa_0'}, dimensions={0}, use_global_device_ids=true | all-gather | bytes 61440 | tf_op jit(solution)/shard_map/all_gather | solution.py:35
  136.2 0.1 fusion.16
  136.3 1.8 all-gather.5
  138.2 11.8 %all-gather.6 = f32[4,3,1024]{2,1,0:T(4,128)S(1)} all-gather(f32[1,3,1024]{2,1,0:T(4,128)S(1)} %maximum_bitcast_fusion.2), channel_id=4, replica_groups=mesh['aa_0'=4,'aa_1'=2,'ba'=4,'col'=8] {'ba'}, dimensions={0}, use_global_device_ids=true | all-gather | bytes 61440 | tf_op jit(solution)/shard_map/all_gather | solution.py:35
  150.1 0.1 fusion.2
  150.2 26.1 %all-gather.7 = f32[8,3,1024]{2,1,0:T(4,128)S(1)} all-gather(f32[1,3,1024]{2,1,0:T(4,128)S(1)} %maximum_bitcast_fusion.3), channel_id=5, replica_groups=mesh['aa_0'=4,'aa_1'=2,'ba'=4,'col'=8] {'col'}, dimensions={0}, use_global_device_ids=true | all-gather | bytes 110592 | tf_op jit(solution)/shard_map/all_gather | solution.py:35
  176.2 0.1 fusion.47
  176.3 1.4 fusion.43
  (11 shorter events, 0.2 us)
Async XLA Ops:
  6.5 27.5 %copy-start = (s32[8,4,32]{2,1,0:T(4,128)S(1)}, s32[8,4,32]{2,1,0:T(4,128)}, u32[]{:S(2)}) copy-start(s32[8,4,32]{2,1,0:T(4,128)} %param.6) | copy-start | bytes 12292
  6.5 101.5 %all-gather.10.cloned.1.call-start = ((), (), s32[]{:S(2)}) async-start(), calls=%async_computation.1 | async-start | bytes 17301504 | tf_op jit(solution)/shard_map/all_gather | solution.py:72
Sparse Core Ops, SparseCore 0:
  34.2 73.8 all-gather.9
where the time goes:
time: 186 us
  blocking collectives  77.4 us (42%)
  waiting for transfers between devices  72 us (39%)
  matrix products  15.5 us (8%)
  between operations  15.4 us (8%)
  local copies, waits for them, and re-layouts  3.1 us (2%)
  other arithmetic  2.39 us (1%)
    all_gather x1, waiting for transfers between devices, body(): lax.all_gather(full_rows, AA_BA, axis=0, tiled=True)  72 us
    all_gather x4, blocking collectives, gathered_once(): both, at, found = (lax.all_gather(jnp.concatenate(lines), axis), 0, {})  51.6 us
    all_to_all x1, blocking collectives, copy_for_each(): return lax.all_to_all(copies, axis, split_axis=0, concat_axis=0, tiled=True)  25.8 us
    dot_general x1, matrix products, body(): jnp.dot(lax.all_gather(full_rows, AA_BA, axis=0, tiled=True), unembed, pr...  15.5 us
  transfers between devices with their start and end apart: 1, of which 1 were waited for; matrix products, arithmetic and copies ran while one was open for 1% of the time, Pallas kernels for 0%

commit v1 on v0

--- a/solution.py
+++ b/solution.py
@@ -69,7 +69,9 @@
     offset = device_index * vocab_part
     full_rows = gather_directly(own_rows, "col", 1)
     logits = jnp.dot(
-        lax.all_gather(full_rows, AA_BA, axis=0, tiled=True),
+        jnp.concatenate(
+            lax.all_to_all(jnp.stack([full_rows] * lax.axis_size(AA_BA)), AA_BA, 0, 0), axis=0
+        ),
         unembed,
         preferred_element_type=jnp.float32,
     )

time: 186 us -> 329 us (1.77)
  waiting for transfers between devices: 72 us -> 216 us
  between operations: 15.4 us -> 1.99 us
  starting transfers between devices: 0.01 us -> 7.8 us
  local copies, waits for them, and re-layouts: 3.1 us -> 8.27 us
    all_to_all x0 -> x1, waiting for transfers between devices: none -> 216 us  [body(): lax.all_to_all(jnp.stack([full_rows] * lax.axis_size(AA_BA)), AA_BA, 0, 0)]
    all_gather x1 -> x0, waiting for transfers between devices: 72 us -> none  [body(): lax.all_gather(full_rows, AA_BA, axis=0, tiled=True)]
    all_to_all x0 -> x1, starting transfers between devices: none -> 7.8 us  [body(): lax.all_to_all(jnp.stack([full_rows] * lax.axis_size(AA_BA)), AA_BA, 0, 0)]
    another operation x0 -> x2, local copies, waits for them, and re-layouts: none -> 6.01 us  [body(): jnp.stack([full_rows] * lax.axis_size(AA_BA))]
  transfers between devices with their start and end apart: 1 -> 1, of which waited for: 1 -> 1; matrix products, arithmetic and copies ran while one was open for 1% -> 0% of each run, Pallas kernels for 0% -> 0%
where the time goes in v1:
time: 329 us; the launch traced here: 327 us
  waiting for transfers between devices  216 us (66%)
  blocking collectives  75.1 us (23%)
  matrix products  15.5 us (5%)
  local copies, waits for them, and re-layouts  8.27 us (3%)
  starting transfers between devices  7.8 us (2%)
    all_to_all x1, waiting for transfers between devices, body(): lax.all_to_all(jnp.stack([full_rows] * lax.axis_size(AA_BA)), AA_BA, 0, 0)  216 us
    all_gather x4, blocking collectives, gathered_once(): both, at, found = (lax.all_gather(jnp.concatenate(lines), axis), 0, {})  49.3 us
    all_to_all x1, blocking collectives, copy_for_each(): return lax.all_to_all(copies, axis, split_axis=0, concat_axis=0, tiled=True)  25.8 us
    dot_general x1, matrix products, body(): jnp.dot(jnp.concatenate(lax.all_to_all(jnp.stack([full_rows] * lax.axis_s...  15.5 us
    all_to_all x1, starting transfers between devices, body(): lax.all_to_all(jnp.stack([full_rows] * lax.axis_size(AA_BA)), AA_BA, 0, 0)  7.8 us
  transfers between devices with their start and end apart: 1, of which 1 were waited for; matrix products, arithmetic and copies ran while one was open for 0% of the time, Pallas kernels for 0%

profile of v1, /device:TPU:2, one launch (start us, length us, event | category | flops | bytes accessed | tf_op | source)
XLA Modules:
  0.0 326.6 jit_solution(11175913170780034391)
XLA Ops:
  0.0 0.9 broadcast_in_dim.18
  0.9 25.8 %all_to_all.10 = bf16[8,32,1024]{2,1,0:T(8,128)(2,1)S(1)} all-to-all(bf16[8,32,1024]{2,1,0:T(8,128)(2,1)S(1)} %broadcast_in_dim.18), channel_id=1, replica_groups=mesh['aa_0'=4,'aa_1'=2,'ba'=4,'col'=8] {'col'}, dimensions={0} | all-to-all | bytes 1048576 | tf_op jit(solution)/shard_map/all_to_all | solution.py:20
  26.7 6.0 %stack.3 = bf16[32,32,8192]{2,1,0:T(8,128)(2,1)} broadcast(bf16[32,8192]{1,0:T(8,128)(2,1)S(1)} %bitcast.217), dimensions={1,2} | broadcast | bytes 17301504 | tf_op jit(solution)/shard_map/stack | solution.py:73
  32.7 0.0 copy-start
  32.7 7.8 %all-to-all-start.1 = ((bf16[32,32,8192]{2,1,0:T(8,128)(2,1)}), bf16[32,32,8192]{2,1,0:T(8,128)(2,1)}, u32[]{:S(2)}, u32[]{:S(2)}) async-start(bf16[32,32,8192]{2,1,0:T(8,128)(2,1)} %stack.3), calls=%async_computation.1 | async-start | bytes 33554432 | tf_op jit(solution)/shard_map/all_to_all | solution.py:73
  40.5 0.0 copy-done
  40.5 0.1 sub.213
  40.6 1.3 dynamic_slice.6
  42.5 215.5 %all-to-all-done.1 = bf16[32,32,8192]{2,1,0:T(8,128)(2,1)} async-done(((bf16[32,32,8192]{2,1,0:T(8,128)(2,1)}), bf16[32,32,8192]{2,1,0:T(8,128)(2,1)}, u32[]{:S(2)}, u32[]{:S(2)}) %all-to-all-start.1) | async-done | bytes 16777248 | tf_op jit(solution)/shard_map/all_to_all | solution.py:73
  258.1 15.5 %fusion.49 = (f32[1024]{0:T(1024)S(1)}, f32[1024,594]{0,1:T(8,128)S(1)}) fusion(bf16[1024,8192]{1,0:T(8,128)(2,1)} %bitcast.3, bf16[8192,594]{0,1:T(8,128)(2,1)} %param.5), kind=kOutput, calls=%fused_computation.97 | convolution fusion | flops 9966273536 | bytes 28946432 | tf_op jit(solution)/shard_map/dot_general | solution.py:71
  273.6 0.7 exponential_reduce_fusion
  274.3 12.2 %all-gather.4 = f32[4,3,1024]{2,1,0:T(4,128)S(1)} all-gather(f32[1,3,1024]{2,1,0:T(4,128)S(1)} %maximum_bitcast_fusion), channel_id=2, replica_groups=mesh['aa_0'=4,'aa_1'=2,'ba'=4,'col'=8] {'aa_0'}, dimensions={0}, use_global_device_ids=true | all-gather | bytes 61440 | tf_op jit(solution)/shard_map/all_gather | solution.py:35
  286.5 0.1 fusion.16
  286.6 1.8 all-gather.5
  288.5 10.7 %all-gather.6 = f32[4,3,1024]{2,1,0:T(4,128)S(1)} all-gather(f32[1,3,1024]{2,1,0:T(4,128)S(1)} %maximum_bitcast_fusion.2), channel_id=4, replica_groups=mesh['aa_0'=4,'aa_1'=2,'ba'=4,'col'=8] {'ba'}, dimensions={0}, use_global_device_ids=true | all-gather | bytes 61440 | tf_op jit(solution)/shard_map/all_gather | solution.py:35
  299.2 0.1 fusion.2
  299.3 24.6 %all-gather.7 = f32[8,3,1024]{2,1,0:T(4,128)S(1)} all-gather(f32[1,3,1024]{2,1,0:T(4,128)S(1)} %maximum_bitcast_fusion.3), channel_id=5, replica_groups=mesh['aa_0'=4,'aa_1'=2,'ba'=4,'col'=8] {'col'}, dimensions={0}, use_global_device_ids=true | all-gather | bytes 110592 | tf_op jit(solution)/shard_map/all_gather | solution.py:35
  323.9 0.1 fusion.47
  324.0 1.4 fusion.43
  (12 shorter events, 0.2 us)
Async XLA Ops:
  32.7 7.8 %copy-start = (s32[8,4,32]{2,1,0:T(4,128)S(1)}, s32[8,4,32]{2,1,0:T(4,128)}, u32[]{:S(2)}) copy-start(s32[8,4,32]{2,1,0:T(4,128)} %param.6) | copy-start | bytes 12292
  32.7 225.4 %all-to-all-start.1 = ((bf16[32,32,8192]{2,1,0:T(8,128)(2,1)}), bf16[32,32,8192]{2,1,0:T(8,128)(2,1)}, u32[]{:S(2)}, u32[]{:S(2)}) async-start(bf16[32,32,8192]{2,1,0:T(8,128)(2,1)} %stack.3), calls=%async_computation.1 | async-start | bytes 33554432 | tf_op jit(solution)/shard_map/all_to_all | solution.py:73
